TPU v7x, 256 devices: a whole 4x4x8 slice. The times are simulated.
256 devices in a mesh: gx: 16 (over z, x_lo), gy: 16 (over y, x_hi, core).
Axes of the slice: x: 4 (x_hi: 2, x_lo: 2; x = x_hi * 2 + x_lo), y: 4, z: 8, core: 2. Of those that a mesh axis runs over, the one named last changes fastest.
Arguments:
- gradient: float32 [2048, 512], P('gx', 'gy'), may hold values from -6 to 6
- stat_old: float32 [2048, 2048], P('gx', 'gy'), may hold values from -1.001 to 1.001, as said below
Outputs:
- statistic: float32 [2048, 2048], P('gx', 'gy')
- inverse_root: float32 [2048, 2048], P('gx', 'gy')
Inputs may be any that keep to these rules, and one draw needn't show every extreme that they name: stat_old is symmetric positive semidefinite with unit diagonal, the Gram matrix of 2048 unit-length rows of 512 entries.
All inputs are finite; a program needn't handle non-finite values.
Results may differ from a plain program's by a relative error of at most 0.0003.
Values sent between devices are 32-bit elements.
A program may use at most 64 MiB of HBM per device.

v0:
```python
import jax
import jax.numpy as jnp
from jax import lax
from jax.sharding import Mesh
from jax.sharding import PartitionSpec as P

GY = ("gy_0", "gy_1", "gy_2")
GX = ("gx_0", "gx_1")
GX_GY = ("gx_0", "gx_1", "gy_0", "gy_1", "gy_2")


def gather_axes(array, axes, dim):
    filled = array
    for number in range(len(axes) - 1, -1, -1):
        filled = lax.all_gather(filled, axes[number], axis=dim, tiled=True)
    return filled


def folded(array, axes, dim, take_in, carry):
    everything = jax.tree.map(lambda part: gather_axes(part, axes, dim), array)
    return take_in(carry, everything, jnp.int32(0))


def spread(array, axes, root):
    array = jnp.where(lax.axis_index(axes) == root, array, jnp.zeros_like(array))
    for axis in axes:
        array = lax.psum(array, axis)
    return array


def over_axes(array, axes):
    for axis in axes:
        array = lax.psum(array, axis)
    return array


def matmul(leading, trailing):
    return jnp.dot(
        leading, trailing, preferred_element_type=jnp.float32, precision=lax.Precision.HIGHEST
    )


def panels(factor_one, factor_two):
    whole_row = lax.all_gather(factor_one, GY, axis=1, tiled=True)

    def accumulate(running, shard_rows, first_row):
        matching = lax.dynamic_slice_in_dim(whole_row, first_row, shard_rows.shape[0], 1)
        return running + matmul(matching, shard_rows)

    empty = jnp.zeros((factor_one.shape[0], factor_two.shape[1]), jnp.float32)
    return folded(factor_two, GX, 0, accumulate, empty)


def product(factor_one, factor_two):
    return panels(factor_one, factor_two)


def local(gradient, stat_old):
    count_rows = lax.axis_size(GX)
    count_cols = lax.axis_size(GY)
    factor = count_rows // count_cols
    piece_width = stat_old.shape[0]
    row_index = lax.axis_index(GX)
    col_index = lax.axis_index(GY)
    panel_rows = lax.all_gather(gradient, GY, axis=1, tiled=True)
    outer_parts = []
    for member in range(factor):
        column_rows = spread(panel_rows, GX, col_index * factor + member)
        outer_parts.append(matmul(panel_rows, column_rows.T))
    outer = jnp.concatenate(outer_parts, axis=1) / panel_rows.shape[1]
    statistic = 0.9 * stat_old + outer
    squares = over_axes(jnp.sum(statistic * statistic), GX_GY)
    divisor = 2.0 * jnp.sqrt(squares / (piece_width * count_rows))
    global_rows = row_index * piece_width + lax.broadcasted_iota(jnp.int32, stat_old.shape, 0)
    global_cols = col_index * (factor * piece_width) + lax.broadcasted_iota(
        jnp.int32, stat_old.shape, 1
    )
    identity = (global_rows == global_cols).astype(jnp.float32)
    normed = statistic / divisor
    first_step = 1.5 * identity - 0.5 * normed
    root_half = product(normed, first_step)
    product_mid = product(first_step, root_half)
    second_step = 1.5 * identity - 0.5 * product_mid
    inverse_root = product(second_step, first_step)
    return (statistic, inverse_root)


def solution(mesh):
    torus = Mesh(mesh.devices.reshape(8, 2, 4, 2, 2), ("gx_0", "gx_1", "gy_0", "gy_1", "gy_2"))
    placed = (P(GX, GY), P(GX, GY))
    return jax.shard_map(
        local, mesh=torus, in_specs=placed, out_specs=(P(GX, GY), P(GX, GY)), check_vma=False
    )
```

profile of v0, /device:TPU:1, one launch (start us, length us, event | category | flops | bytes accessed | tf_op | source)
XLA Modules:
  0.0 435.5 jit_solution(8363940582427046131)
XLA Ops:
  7.2 0.7 copy-done.3
  7.9 26.8 %all_gather.26 = f32[128,512]{0,1:T(8,128)S(1)} all-gather(f32[128,32]{0,1:T(8,128)S(1)} %copy-done.3), channel_id=1, replica_groups=mesh['gx_0'=8,'gx_1'=2,'gy_0'=4,'gy_1'=2,'gy_2'=2] {'gy_0','gy_1','gy_2'}, dimensions={1}, use_global_device_ids=true | all-gather | bytes 278528 | tf_op jit(solution)/shard_map/all_gather | solution.py:65
  34.6 0.7 broadcast_select_fusion
  35.4 65.4 %all-reduce.3.cloned.1.call-done = f32[128,512]{0,1:T(8,128)} async-done(((f32[128,512]{0,1:T(8,128)}), f32[128,512]{0,1:T(8,128)}) %all-reduce.3.cloned.1.call-update) | async-done | bytes 262160 | tf_op jit(solution)/shard_map/psum | solution.py:27
  100.9 0.8 copy-done.2
  101.7 39.7 %all-reduce.5.cloned.1.call-done = f32[128,512]{0,1:T(8,128)} async-done(((f32[128,512]{0,1:T(8,128)}), f32[128,512]{0,1:T(8,128)}) %all-reduce.5.cloned.1.call-update) | async-done | bytes 262160 | tf_op jit(solution)/shard_map/psum | solution.py:27
  141.4 2.1 multiply_reduce_fusion
  143.6 14.6 %psum.51 = f32[]{:T(128)} all-reduce(f32[]{:T(128)} %get-tuple-element.6), channel_id=1, replica_groups=mesh['gx_0'=8,'gx_1'=2,'gy_0'=4,'gy_1'=2,'gy_2'=2] {'gx_0'}, use_global_device_ids=true, to_apply=%region_3.4 | all-reduce | flops 1 | bytes 8 | tf_op jit(solution)/shard_map/psum | solution.py:33
  158.1 4.4 %psum.52 = f32[]{:T(128)} all-reduce(f32[]{:T(128)} %psum.51), channel_id=1, replica_groups=mesh['gx_0'=8,'gx_1'=2,'gy_0'=4,'gy_1'=2,'gy_2'=2] {'gx_1'}, use_global_device_ids=true, to_apply=%region_4.5 | all-reduce | flops 1 | bytes 8 | tf_op jit(solution)/shard_map/psum | solution.py:33
  162.5 9.1 %psum.53 = f32[]{:T(128)} all-reduce(f32[]{:T(128)} %psum.52), channel_id=1, replica_groups=mesh['gx_0'=8,'gx_1'=2,'gy_0'=4,'gy_1'=2,'gy_2'=2] {'gy_0'}, use_global_device_ids=true, to_apply=%region_5.6 | all-reduce | flops 1 | bytes 8 | tf_op jit(solution)/shard_map/psum | solution.py:33
  171.6 5.9 %psum.54 = f32[]{:T(128)} all-reduce(f32[]{:T(128)} %psum.53), channel_id=1, replica_groups=mesh['gx_0'=8,'gx_1'=2,'gy_0'=4,'gy_1'=2,'gy_2'=2] {'gy_1'}, use_global_device_ids=true, to_apply=%region_6.7 | all-reduce | flops 1 | bytes 8 | tf_op jit(solution)/shard_map/psum | solution.py:33
  177.5 11.8 %psum.55 = f32[]{:T(128)} all-reduce(f32[]{:T(128)} %psum.54), channel_id=1, replica_groups=mesh['gx_0'=8,'gx_1'=2,'gy_0'=4,'gy_1'=2,'gy_2'=2] {'gy_2'}, use_global_device_ids=true, to_apply=%region_7.8 | all-reduce | flops 1 | bytes 8 | tf_op jit(solution)/shard_map/psum | solution.py:33
  190.0 0.6 select_subtract_fusion
  190.6 3.9 all_gather.29
  195.7 29.4 %all-gather.10.cloned.1.call-done = f32[2048,128]{0,1:T(8,128)} async-done(((f32[256,128]{0,1:T(8,128)}), f32[2048,128]{0,1:T(8,128)}) %all-gather.10.cloned.1.call-update) | async-done | bytes 1048592 | tf_op jit(solution)/shard_map/all_gather | solution.py:15
  225.1 56.8 %all-gather.8.cloned.1.call-done = f32[128,2048]{0,1:T(8,128)} async-done(((f32[128,128]{0,1:T(8,128)}), f32[128,2048]{0,1:T(8,128)}) %all-gather.8.cloned.1.call-update) | async-done | bytes 1048592 | tf_op jit(solution)/shard_map/all_gather | solution.py:44
  281.9 3.4 fusion.3
  285.2 3.9 all_gather.31
  289.2 44.5 %all-gather.6.cloned.1.call-done = f32[128,2048]{0,1:T(8,128)} async-done(((f32[128,128]{0,1:T(8,128)}), f32[128,2048]{0,1:T(8,128)}) %all-gather.6.cloned.1.call-update) | async-done | bytes 1048592 | tf_op jit(solution)/shard_map/all_gather | solution.py:44
  333.7 33.6 %all-gather.12.cloned.1.call-done = f32[2048,128]{1,0:T(8,128)} async-done(((f32[256,128]{1,0:T(8,128)}), f32[2048,128]{1,0:T(8,128)}) %all-gather.12.cloned.1.call-update) | async-done | bytes 1048592 | tf_op jit(solution)/shard_map/all_gather | solution.py:15
  367.3 4.0 fusion
  371.3 0.7 copy.5
  372.0 53.0 %all-gather.14.cloned.1.call-done = f32[128,2048]{0,1:T(8,128)} async-done(((f32[128,128]{0,1:T(8,128)}), f32[128,2048]{0,1:T(8,128)}) %all-gather.14.cloned.1.call-update) | async-done | bytes 1048592 | tf_op jit(solution)/shard_map/all_gather | solution.py:44
  425.0 3.7 fusion.4
  (22 shorter events, 1.5 us)
Async XLA Ops:
  7.2 0.7 copy-start.3
  7.2 93.6 %all-reduce.3.cloned.1.call-start = ((), (), s32[]{:S(2)}) async-start(), calls=%async_computation | async-start | bytes 524288 | tf_op jit(solution)/shard_map/psum | solution.py:27
  35.4 106.1 %all-reduce.5.cloned.1.call-start = ((), (), s32[]{:S(2)}) async-start(), calls=%async_computation.1 | async-start | bytes 524288 | tf_op jit(solution)/shard_map/psum | solution.py:27
  100.8 0.8 copy-start.2
  100.8 124.2 %all-gather.10.cloned.1.call-start = ((), (), s32[]{:S(2)}) async-start(), calls=%async_computation.4 | async-start | bytes 1179648 | tf_op jit(solution)/shard_map/all_gather | solution.py:15
  190.6 3.9 copy-start.1
  194.5 87.3 %all-gather.8.cloned.1.call-start = ((), (), s32[]{:S(2)}) async-start(), calls=%async_computation.3 | async-start | bytes 1114112 | tf_op jit(solution)/shard_map/all_gather | solution.py:44
  195.1 138.6 %all-gather.6.cloned.1.call-start = ((), (), s32[]{:S(2)}) async-start(), calls=%async_computation.2 | async-start | bytes 1114112 | tf_op jit(solution)/shard_map/all_gather | solution.py:44
  195.7 171.6 %all-gather.12.cloned.1.call-start = ((), (), s32[]{:S(2)}) async-start(), calls=%async_computation.5 | async-start | bytes 1179648 | tf_op jit(solution)/shard_map/all_gather | solution.py:15
  289.1 135.9 %copy-start = (f32[2048,128]{0,1:T(8,128)S(1)}, f32[2048,128]{0,1:T(8,128)}, u32[]{:S(2)}) copy-start(f32[2048,128]{0,1:T(8,128)} %all-gather.10.cloned.1.call-done) | copy-start | bytes 3145732
  289.1 135.9 %all-gather.14.cloned.1.call-start = ((), (), s32[]{:S(2)}) async-start(), calls=%async_computation.6 | async-start | bytes 1114112 | tf_op jit(solution)/shard_map/all_gather | solution.py:44
Sparse Core Ops, SparseCore 0:
  35.5 65.2 all-reduce.2
  103.4 38.0 all-reduce.4
  194.6 30.4 all-gather.9
  228.3 53.5 all-gather.7
  285.0 48.6 all-gather.5
  335.4 31.8 all-gather.11
  371.4 53.5 all-gather.13
where the time goes:
time: 436 us
  waiting for transfers between devices  323 us (74%)
  blocking collectives  80.2 us (18%)
  between operations  14.9 us (3%)
  matrix products  13.2 us (3%)
    all_gather x3, waiting for transfers between devices, panels(): whole_row = lax.all_gather(factor_one, GY, axis=1, tiled=True)  154 us
    psum x2, waiting for transfers between devices, spread(): array = lax.psum(array, axis)  105 us
    all_gather x2, waiting for transfers between devices, gather_axes(): filled = lax.all_gather(filled, axes[number], axis=dim, tiled=True)  62.9 us
    psum x5, blocking collectives, over_axes(): array = lax.psum(array, axis)  45.7 us
    all_gather x1, blocking collectives, local(): panel_rows = lax.all_gather(gradient, GY, axis=1, tiled=True)  26.8 us
    dot_general x4, matrix products, matmul(): jnp.dot(leading, trailing, preferred_element_type=jnp.float32, precision=...  13.2 us
  transfers between devices with their start and end apart: 7, of which 7 were waited for; matrix products, arithmetic and copies ran while one was open for 1% of the time, Pallas kernels for 0%

commit v1 on v0

--- a/solution.py
+++ b/solution.py
@@ -24,7 +24,7 @@
 def spread(array, axes, root):
     array = jnp.where(lax.axis_index(axes) == root, array, jnp.zeros_like(array))
     for axis in axes:
-        array = lax.psum(array, axis)
+        array = jnp.sum(lax.all_gather(array, axis), 0)
     return array
 
 

time: 436 us -> 382 us (0.88)
  waiting for transfers between devices: 323 us -> 258 us
  blocking collectives: 80.2 us -> 90.6 us
    psum x2 -> x0, waiting for transfers between devices: 105 us -> none  [spread(): array = lax.psum(array, axis)]
    all_gather x0 -> x1, waiting for transfers between devices: none -> 39.5 us  [spread(): array = jnp.sum(lax.all_gather(array, axis), 0)]
    all_gather x0 -> x1, blocking collectives: none -> 5.89 us  [spread(): array = jnp.sum(lax.all_gather(array, axis), 0)]
  transfers between devices with their start and end apart: 7 -> 6, of which waited for: 7 -> 6; matrix products, arithmetic and copies ran while one was open for 1% -> 1% of each run, Pallas kernels for 0% -> 0%
where the time goes in v1:
time: 382 us
  waiting for transfers between devices  258 us (68%)
  blocking collectives  90.6 us (24%)
  between operations  14.9 us (4%)
  matrix products  12.2 us (3%)
  local copies, waits for them, and re-layouts  3.99 us (1%)
    all_gather x3, waiting for transfers between devices, panels(): whole_row = lax.all_gather(factor_one, GY, axis=1, tiled=True)  154 us
    all_gather x2, waiting for transfers between devices, gather_axes(): filled = lax.all_gather(filled, axes[number], axis=dim, tiled=True)  62.4 us
    psum x5, blocking collectives, over_axes(): array = lax.psum(array, axis)  49.9 us
    all_gather x1, waiting for transfers between devices, spread(): array = jnp.sum(lax.all_gather(array, axis), 0)  39.5 us
    all_gather x1, blocking collectives, local(): panel_rows = lax.all_gather(gradient, GY, axis=1, tiled=True)  27 us
    dot_general x4, matrix products, matmul(): jnp.dot(leading, trailing, preferred_element_type=jnp.float32, precision=...  12.2 us
    all_gather x2, blocking collectives, gather_axes(): filled = lax.all_gather(filled, axes[number], axis=dim, tiled=True)  7.76 us
  transfers between devices with their start and end apart: 6, of which 6 were waited for; matrix products, arithmetic and copies ran while one was open for 1% of the time, Pallas kernels for 0%

profile of v1, /device:TPU:1, one launch (start us, length us, event | category | flops | bytes accessed | tf_op | source)
XLA Modules:
  0.0 382.0 jit_solution(9099397590832761059)
XLA Ops:
  7.2 27.0 %all_gather.38 = f32[128,512]{0,1:T(8,128)S(1)} all-gather(f32[128,32]{0,1:T(8,128)} %param.2), channel_id=1, replica_groups=mesh['gx_0'=8,'gx_1'=2,'gy_0'=4,'gy_1'=2,'gy_2'=2] {'gy_0','gy_1','gy_2'}, dimensions={1}, use_global_device_ids=true | all-gather | bytes 278528 | tf_op jit(solution)/shard_map/all_gather | solution.py:65
  34.2 0.7 broadcast_select_fusion
  35.0 0.9 copy.8
  36.0 39.5 %all-gather.19.cloned.1.call-done = f32[1024,512]{0,1:T(8,128)} async-done(((f32[128,512]{0,1:T(8,128)}), f32[1024,512]{0,1:T(8,128)}) %all-gather.19.cloned.1.call-update) | async-done | bytes 2097168 | tf_op jit(solution)/shard_map/all_gather | solution.py:27
  75.5 2.1 copy.12
  78.1 5.9 %all-gather.1 = f32[256,512]{0,1:T(8,128)S(1)} all-gather(f32[128,512]{0,1:T(8,128)S(1)} %bitcast_reduce_fusion), channel_id=3, replica_groups=mesh['gx_0'=8,'gx_1'=2,'gy_0'=4,'gy_1'=2,'gy_2'=2] {'gx_1'}, dimensions={0}, use_global_device_ids=true | all-gather | bytes 786432 | tf_op jit(solution)/shard_map/all_gather | solution.py:27
  84.9 1.2 multiply_reduce_fusion
  86.1 13.3 %psum.35 = f32[]{:T(128)} all-reduce(f32[]{:T(128)} %get-tuple-element.10), channel_id=1, replica_groups=mesh['gx_0'=8,'gx_1'=2,'gy_0'=4,'gy_1'=2,'gy_2'=2] {'gx_0'}, use_global_device_ids=true, to_apply=%region_3.4 | all-reduce | flops 1 | bytes 8 | tf_op jit(solution)/shard_map/psum | solution.py:33
  99.3 4.4 %psum.36 = f32[]{:T(128)} all-reduce(f32[]{:T(128)} %psum.35), channel_id=1, replica_groups=mesh['gx_0'=8,'gx_1'=2,'gy_0'=4,'gy_1'=2,'gy_2'=2] {'gx_1'}, use_global_device_ids=true, to_apply=%region_4.5 | all-reduce | flops 1 | bytes 8 | tf_op jit(solution)/shard_map/psum | solution.py:33
  103.7 9.4 %psum.37 = f32[]{:T(128)} all-reduce(f32[]{:T(128)} %psum.36), channel_id=1, replica_groups=mesh['gx_0'=8,'gx_1'=2,'gy_0'=4,'gy_1'=2,'gy_2'=2] {'gy_0'}, use_global_device_ids=true, to_apply=%region_5.6 | all-reduce | flops 1 | bytes 8 | tf_op jit(solution)/shard_map/psum | solution.py:33
  113.1 5.9 %psum.38 = f32[]{:T(128)} all-reduce(f32[]{:T(128)} %psum.37), channel_id=1, replica_groups=mesh['gx_0'=8,'gx_1'=2,'gy_0'=4,'gy_1'=2,'gy_2'=2] {'gy_1'}, use_global_device_ids=true, to_apply=%region_6.7 | all-reduce | flops 1 | bytes 8 | tf_op jit(solution)/shard_map/psum | solution.py:33
  119.0 17.1 %psum.39 = f32[]{:T(128)} all-reduce(f32[]{:T(128)} %psum.38), channel_id=1, replica_groups=mesh['gx_0'=8,'gx_1'=2,'gy_0'=4,'gy_1'=2,'gy_2'=2] {'gy_2'}, use_global_device_ids=true, to_apply=%region_7.8 | all-reduce | flops 1 | bytes 8 | tf_op jit(solution)/shard_map/psum | solution.py:33
  137.4 3.9 %all_gather.45 = f32[256,128]{0,1:T(8,128)} all-gather(f32[128,128]{0,1:T(8,128)S(1)} %get-tuple-element.8), channel_id=1, replica_groups=mesh['gx_0'=8,'gx_1'=2,'gy_0'=4,'gy_1'=2,'gy_2'=2] {'gx_1'}, dimensions={0}, use_global_device_ids=true | all-gather | bytes 196608 | tf_op jit(solution)/shard_map/all_gather | solution.py:15
  141.3 0.7 all-gather.11.cloned.1.call-update
  142.6 28.8 %all-gather.13.cloned.1.call-done = f32[2048,128]{0,1:T(8,128)} async-done(((f32[256,128]{0,1:T(8,128)}), f32[2048,128]{0,1:T(8,128)}) %all-gather.13.cloned.1.call-update) | async-done | bytes 1048592 | tf_op jit(solution)/shard_map/all_gather | solution.py:15
  171.4 56.9 %all-gather.11.cloned.1.call-done = f32[128,2048]{0,1:T(8,128)} async-done(((f32[128,128]{0,1:T(8,128)}), f32[128,2048]{0,1:T(8,128)}) %all-gather.11.cloned.1.call-update) | async-done | bytes 1048592 | tf_op jit(solution)/shard_map/all_gather | solution.py:44
  228.4 3.4 fusion.3
  231.7 3.9 %all_gather.47 = f32[256,128]{1,0:T(8,128)} all-gather(f32[128,128]{1,0:T(8,128)S(1)} %fusion.3), channel_id=1, replica_groups=mesh['gx_0'=8,'gx_1'=2,'gy_0'=4,'gy_1'=2,'gy_2'=2] {'gx_1'}, dimensions={0}, use_global_device_ids=true | all-gather | bytes 196608 | tf_op jit(solution)/shard_map/all_gather | solution.py:15
  235.7 44.5 %all-gather.9.cloned.1.call-done = f32[128,2048]{0,1:T(8,128)} async-done(((f32[128,128]{0,1:T(8,128)}), f32[128,2048]{0,1:T(8,128)}) %all-gather.9.cloned.1.call-update) | async-done | bytes 1048592 | tf_op jit(solution)/shard_map/all_gather | solution.py:44
  280.2 33.6 %all-gather.15.cloned.1.call-done = f32[2048,128]{1,0:T(8,128)} async-done(((f32[256,128]{1,0:T(8,128)}), f32[2048,128]{1,0:T(8,128)}) %all-gather.15.cloned.1.call-update) | async-done | bytes 1048592 | tf_op jit(solution)/shard_map/all_gather | solution.py:15
  313.8 4.0 %fusion = f32[128,128]{0,1:T(8,128)} fusion(f32[128,2048]{0,1:T(8,128)} %all-gather.9.cloned.1.call-done, f32[2048,128]{1,0:T(8,128)} %all-gather.15.cloned.1.call-done, s32[128]{0:T(128)S(1)} %get-tuple-element.13, s32[128]{0:T(128)S(1)} %get-tuple-element.12), kind=kOutput, calls=%fused_computation.2 | convolution fusion | flops 402718720 | bytes 2163712 | tf_op jit(solution)/shard_map/dot_general | solution.py:38
  317.8 0.7 copy.10
  318.5 53.0 %all-gather.17.cloned.1.call-done = f32[128,2048]{0,1:T(8,128)} async-done(((f32[128,128]{0,1:T(8,128)}), f32[128,2048]{0,1:T(8,128)}) %all-gather.17.cloned.1.call-update) | async-done | bytes 1048592 | tf_op jit(solution)/shard_map/all_gather | solution.py:44
  371.5 3.7 fusion.4
  (20 shorter events, 2.9 us)
Async XLA Ops:
  7.2 68.3 %all-gather.19.cloned.1.call-start = ((), (), s32[]{:S(2)}) async-start(), calls=%async_computation.5 | async-start | bytes 2359296 | tf_op jit(solution)/shard_map/all_gather | solution.py:27
  35.0 136.4 %all-gather.13.cloned.1.call-start = ((), (), s32[]{:S(2)}) async-start(), calls=%async_computation.2 | async-start | bytes 1179648 | tf_op jit(solution)/shard_map/all_gather | solution.py:15
  137.4 4.7 %copy-start.1 = (f32[128,128]{0,1:T(8,128)}, f32[128,128]{0,1:T(8,128)S(1)}, u32[]{:S(2)}) copy-start(f32[128,128]{0,1:T(8,128)S(1)} %get-tuple-element.8) | copy-start | bytes 196612
  141.3 87.1 %all-gather.11.cloned.1.call-start = ((), (), s32[]{:S(2)}) async-start(), calls=%async_computation.1 | async-start | bytes 1114112 | tf_op jit(solution)/shard_map/all_gather | solution.py:44
  142.0 138.2 %all-gather.9.cloned.1.call-start = ((), (), s32[]{:S(2)}) async-start(), calls=%async_computation | async-start | bytes 1114112 | tf_op jit(solution)/shard_map/all_gather | solution.py:44
  142.6 171.2 %all-gather.15.cloned.1.call-start = ((), (), s32[]{:S(2)}) async-start(), calls=%async_computation.3 | async-start | bytes 1179648 | tf_op jit(solution)/shard_map/all_gather | solution.py:15
  171.4 200.1 %copy-start = (f32[2048,128]{0,1:T(8,128)S(1)}, f32[2048,128]{0,1:T(8,128)}, u32[]{:S(2)}) copy-start(f32[2048,128]{0,1:T(8,128)} %all-gather.13.cloned.1.call-done) | copy-start | bytes 3145732
  235.6 135.9 %all-gather.17.cloned.1.call-start = ((), (), s32[]{:S(2)}) async-start(), calls=%async_computation.4 | async-start | bytes 1114112 | tf_op jit(solution)/shard_map/all_gather | solution.py:44
Sparse Core Ops, SparseCore 0:
  35.1 40.3 all-gather.18
  141.4 29.9 all-gather.12
  174.8 53.5 all-gather.10
  231.5 48.6 all-gather.8
  281.9 31.8 all-gather.14
  317.9 53.5 all-gather.16
